TPU v7x, 32 devices: a whole 2x2x4 slice. The times are simulated.
32 devices in a mesh: shot: 4 (over y, core), tile: 8 (over z, x).
Axes of the slice: x: 2, y: 2, z: 4, core: 2. Of those that a mesh axis runs over, the one named last changes fastest.
Arguments:
- source: bfloat16 [64, 1, 32, 32, 128], P(('shot', 'tile')), may hold values from -6 to 6
- receiver: bfloat16 [64, 1, 32, 32, 128], P(('shot', 'tile')), may hold values from -6 to 6
- corners: int32 [64, 2], P(('shot', 'tile')), may hold values from 0 to 224, as said below
Outputs:
- filtered: float32 [32, 256, 256], P('tile', 'shot')
Inputs may be any that keep to these rules, and one draw needn't show every extreme that they name: corners[s, 0] is at most 224 and corners[s, 1] at most 128, so every box lies inside the image.
All inputs are finite; a program needn't handle non-finite values.
Results may differ from a plain program's by a relative error of at most 0.0003.
Values may be sent and summed in bfloat16 or wider, within the bound.
A program may use at most 64 MiB of HBM per device.

v0:
```python
import functools

import jax
import jax.numpy as jnp
from jax import lax
from jax.experimental import pallas as pl
from jax.experimental.pallas import tpu as pltpu
from jax.sharding import PartitionSpec as P

X = 256
Y = 256
LANES = 128

damping = 1.0


def partner(index, k, count):
    if count & (count - 1):
        return lax.rem(index + k, count)
    bit = 1
    result = index
    while bit < count:
        if k & bit:
            result = result + bit * (1 - 2 * lax.rem(index // bit, 2))
        bit *= 2
    return result


def plane_order(depth):
    if depth < 3:
        return list(range(depth))
    return [0, depth - 1] + list(range(1, depth - 1))


def kernel(
    ns, nt, src, rcv, cor, out, sbuf, rx, cbuf, csm, boxes, acc, r1, r2, nrm, hx, hz, rows, lap,
    in_sem, out_sem, rx_send, rx_recv, c_send, c_recv, c_local,
    s1_send, s1_recv, s2_send, s2_recv, row_send, row_recv, face_send, face_recv,
):
    depth, strip, width = nrm.shape
    spd, samples = src.shape[0], src.shape[1]
    box_rows = src.shape[3]
    halves = width // LANES
    order = plane_order(depth)
    shots = nt * spd
    block = min(box_rows, strip)
    per_strip = strip // block
    half_ns = ns // 2
    shot = lax.axis_index("shot")
    tile = lax.axis_index("tile")
    core = lax.rem(shot, 2)
    pair = shot // 2
    other = 1 - core

    barrier = pltpu.get_barrier_semaphore()
    for k in range(1, ns):
        pl.semaphore_signal(barrier, inc=1, device_id={"shot": lax.rem(shot + k, ns)})
    for k in range(1, nt):
        pl.semaphore_signal(barrier, inc=1, device_id={"tile": lax.rem(tile + k, nt)})

    for w, ref in enumerate((src, rcv)):
        for i in range(spd):
            for n in range(samples):
                pltpu.make_async_copy(ref.at[i, n], sbuf.at[:, w, i, n], in_sem).start()
    pltpu.make_async_copy(cor, cbuf.at[tile], c_recv).start()
    for p in order:
        for w, ref in enumerate((src, rcv)):
            pltpu.make_async_copy(ref.at[:, :, tile * depth + p], rx.at[p, tile, w], rx_recv.at[p]).start()
    pltpu.make_async_copy(sbuf, sbuf, in_sem).wait()

    pl.semaphore_wait(barrier, ns - 1 + nt - 1)

    for p in order:
        for k in range(nt - 1, 0, -1):
            to = partner(tile, k, nt)
            if p == order[0]:
                pltpu.make_async_remote_copy(
                    src_ref=cor, dst_ref=cbuf.at[tile], send_sem=c_send, recv_sem=c_recv, device_id={"tile": to}
                ).start()
            pltpu.make_async_remote_copy(
                src_ref=sbuf.at[to * depth + p],
                dst_ref=rx.at[p, tile],
                send_sem=rx_send.at[p],
                recv_sem=rx_recv.at[p],
                device_id={"tile": to},
            ).start()

    edges = (
        (shot < ns - 1, shot > 0, {"shot": lax.rem(shot + 1, ns)}),
        (shot > 0, shot < ns - 1, {"shot": lax.rem(shot + ns - 1, ns)}),
    )
    faces = (
        (tile < nt - 1, tile > 0, {"tile": lax.rem(tile + 1, nt)}, depth - 1),
        (tile > 0, tile < nt - 1, {"tile": lax.rem(tile + nt - 1, nt)}, 0),
    )
    for d in range(2):
        @pl.when(jnp.logical_not(edges[d][1]))
        def _(d=d):
            hx[d] = jnp.zeros((depth, 1, width), jnp.float32)

        @pl.when(jnp.logical_not(faces[d][1]))
        def _(d=d):
            hz[d] = jnp.zeros((strip, width), jnp.float32)

    def edge_copy(d, p):
        return pltpu.make_async_remote_copy(
            src_ref=rows.at[d, p], dst_ref=hx.at[d, p],
            send_sem=row_send.at[d, p], recv_sem=row_recv.at[d, p], device_id=edges[d][2],
        )

    def face_copy(d):
        return pltpu.make_async_remote_copy(
            src_ref=nrm.at[faces[d][3]], dst_ref=hz.at[d],
            send_sem=face_send.at[d], recv_sem=face_recv.at[d], device_id=faces[d][2],
        )

    zero = jnp.zeros((block, LANES), jnp.float32)

    def clear(s, carry):
        for q in range(2):
            for h in range(halves):
                boxes[s, q, h, pl.ds(0, block), :] = zero
                boxes[s, q, h, pl.ds(block + box_rows, block), :] = zero
        return carry

    lax.fori_loop(0, shots, clear, 0)

    pltpu.make_async_copy(cbuf, cbuf, c_recv).wait()
    to_scalar = pltpu.make_async_copy(cbuf, csm, c_local)
    to_scalar.start()
    to_scalar.wait()

    lane = lax.broadcasted_iota(jnp.int32, (box_rows, LANES), 1)

    def expand(p):
        def peer(t, carry):
            for i in range(spd):
                s = t * spd + i
                col = csm[t, i, 1]
                turn = lax.rem(col, LANES)
                image = jnp.zeros((box_rows, LANES), jnp.float32)
                light = image
                for n in range(samples):
                    wave = rx[p, t, 0, i, n].astype(jnp.float32)
                    back = rx[p, t, 1, i, n].astype(jnp.float32)
                    image = wave * back if n == 0 else image + wave * back
                    light = wave * wave if n == 0 else light + wave * wave
                image = pltpu.roll(image, turn, 1)
                light = pltpu.roll(light, turn, 1)
                for h in range(halves):
                    at = lane + (h * LANES - col)
                    inside = (at >= 0) & (at < LANES)
                    boxes[s, 0, h, pl.ds(block, box_rows), :] = jnp.where(inside, image, 0.0)
                    boxes[s, 1, h, pl.ds(block, box_rows), :] = jnp.where(inside, light, 0.0)
            return carry

        lax.fori_loop(0, nt, peer, 0)

    def place(p, parity):
        def one(n, carry):
            j = 2 * (n // per_strip) + parity
            base = lax.rem(n, per_strip) * block
            first = j * strip + base + block
            total = [[None] * halves for _ in range(2)]
            for s in range(shots):
                start = jnp.clip(first - csm[s // spd, s % spd, 0], 0, box_rows + block)
                for q in range(2):
                    for h in range(halves):
                        piece = boxes[s, q, h, pl.ds(start, block), :]
                        total[q][h] = piece if s == 0 else total[q][h] + piece
            for q in range(2):
                for h in range(halves):
                    acc[p, j, q, pl.ds(base, block), pl.ds(h * LANES, LANES)] = total[q][h]
            return carry

        lax.fori_loop(0, half_ns * per_strip, one, 0)

    def stage1(p):
        for i in range(half_ns):
            pltpu.make_async_remote_copy(
                src_ref=acc.at[p, 2 * i + other],
                dst_ref=r1.at[p, i],
                send_sem=s1_send.at[p],
                recv_sem=s1_recv.at[p],
                device_id={"shot": 2 * pair + other},
            ).start()

    def stage2(p):
        pltpu.make_async_copy(r1.at[p], r1.at[p], s1_recv.at[p]).wait()
        for k in range(1, half_ns):
            to = lax.rem(pair + k, half_ns)
            j = 2 * to + core
            acc[p, j] = acc[p, j] + r1[p, to]
            pltpu.make_async_remote_copy(
                src_ref=acc.at[p, j],
                dst_ref=r2.at[p, k - 1],
                send_sem=s2_send.at[p],
                recv_sem=s2_recv.at[p],
                device_id={"shot": j},
            ).start()

    def finish(p):
        pltpu.make_async_copy(r2.at[p], r2.at[p], s2_recv.at[p]).wait()
        image = acc[p, shot, 0] + r1[p, pair, 0]
        light = acc[p, shot, 1] + r1[p, pair, 1]
        for k in range(half_ns - 1):
            image = image + r2[p, k, 0]
            light = light + r2[p, k, 1]
        normal = image / (damping + light)
        nrm[p] = normal
        rows[0, p] = normal[strip - 1 :, :]
        rows[1, p] = normal[:1, :]
        for d in range(2):
            @pl.when(edges[d][0])
            def _(d=d):
                edge_copy(d, p).start()

            if p == faces[d][3]:
                @pl.when(faces[d][0])
                def _(d=d):
                    face_copy(d).start()

    row = lax.broadcasted_iota(jnp.int32, (strip, width), 0)
    column = lax.broadcasted_iota(jnp.int32, (strip, width), 1)

    def lateral(p):
        center = nrm[p]
        before = jnp.where(row == 0, 0.0, pltpu.roll(center, 1, 0))
        after = jnp.where(row == strip - 1, 0.0, pltpu.roll(center, strip - 1, 0))
        left = jnp.where(column == 0, 0.0, pltpu.roll(center, 1, 1))
        right = jnp.where(column == width - 1, 0.0, pltpu.roll(center, width - 1, 1))
        return before + after + left + right - 6.0 * center

    def wait_edges(p):
        for d in range(2):
            @pl.when(edges[d][1])
            def _(d=d):
                edge_copy(d, p).wait_recv()

    def add_edges(p):
        lap[p, pl.ds(0, 1), :] = lap[p, pl.ds(0, 1), :] + hx[0, p]
        lap[p, pl.ds(strip - 1, 1), :] = lap[p, pl.ds(strip - 1, 1), :] + hx[1, p]

    def emit(p):
        pltpu.make_async_copy(lap.at[p], out.at[p], out_sem.at[p]).start()

    for n, p in enumerate(order):
        pltpu.make_async_copy(rx.at[p], rx.at[p], rx_recv.at[p]).wait()
        expand(p)
        place(p, other)
        stage1(p)
        place(p, core)
        if n >= 1:
            stage2(order[n - 1])
        if n >= 2:
            finish(order[n - 2])
    last = order[-1]
    stage2(last)
    if depth >= 2:
        finish(order[-2])
    early = order[:-1]
    for d in range(2):
        if faces[d][3] != last:
            @pl.when(faces[d][1])
            def _(d=d):
                face_copy(d).wait_recv()
    for p in early:
        value = lateral(p)
        for near, d in ((p - 1, 0), (p + 1, 1)):
            if 0 <= near < depth:
                if near != last:
                    value = value + nrm[near]
            elif faces[d][3] != last:
                value = value + hz[d]
        lap[p] = value
        wait_edges(p)
        add_edges(p)
        if abs(p - last) > 1 and depth >= 3:
            emit(p)
    finish(last)
    for p in early:
        if abs(p - last) == 1:
            lap[p] = lap[p] + nrm[last]
            if depth >= 3:
                emit(p)
    value = lateral(last)
    for near in (last - 1, last + 1):
        if 0 <= near < depth:
            value = value + nrm[near]
    lap[last] = value
    for d in range(2):
        if faces[d][3] == last:
            @pl.when(faces[d][1])
            def _(d=d):
                face_copy(d).wait_recv()

    if depth < 3:
        for d, p in ((0, 0), (1, depth - 1)):
            if faces[d][3] == last or p == last:
                lap[p] = lap[p] + hz[d]
        for p in early:
            emit(p)
    wait_edges(last)
    add_edges(last)
    emit(last)
    for p in order:
        pltpu.make_async_copy(lap.at[p], out.at[p], out_sem.at[p]).wait()

    for d in range(2):
        @pl.when(edges[d][0])
        def _(d=d):
            for p in range(depth):
                edge_copy(d, p).wait_send()

        @pl.when(faces[d][0])
        def _(d=d):
            face_copy(d).wait_send()

    sent = cbuf.at[pl.ds(0, nt - 1)]
    pltpu.make_async_copy(sent, sent, c_send).wait()
    for p in range(depth):
        sent = rx.at[p, pl.ds(0, nt - 1)]
        pltpu.make_async_copy(sent, sent, rx_send.at[p]).wait()
        pltpu.make_async_copy(r1.at[p], r1.at[p], s1_send.at[p]).wait()
        pltpu.make_async_copy(r2.at[p], r2.at[p], s2_send.at[p]).wait()


def solution(mesh):
    ns, nt = mesh.shape["shot"], mesh.shape["tile"]

    def step(source, receiver, corners):
        spd, samples, full_depth, box_rows, box_cols = source.shape
        depth = full_depth // nt
        strip = X // ns
        block = min(box_rows, strip)
        half_ns = ns // 2
        vmem = pltpu.VMEM
        dma = pltpu.SemaphoreType.DMA
        f32 = jnp.float32
        return pl.pallas_call(
            functools.partial(kernel, ns, nt),
            out_shape=jax.ShapeDtypeStruct((depth, strip, Y), f32),
            in_specs=[pl.BlockSpec(memory_space=pl.ANY)] * 3,
            out_specs=pl.BlockSpec(memory_space=pl.ANY),
            scratch_shapes=[
                vmem((full_depth, 2, spd, samples, box_rows, box_cols), jnp.bfloat16),
                vmem((depth, nt, 2, spd, samples, box_rows, box_cols), jnp.bfloat16),
                vmem((nt, spd, 2), jnp.int32),
                pltpu.SMEM((nt, spd, 2), jnp.int32),
                vmem((nt * spd, 2, Y // LANES, box_rows + 2 * block, LANES), f32),
                vmem((depth, ns, 2, strip, Y), f32),
                vmem((depth, half_ns, 2, strip, Y), f32),
                vmem((depth, half_ns - 1, 2, strip, Y), f32),
                vmem((depth, strip, Y), f32),
                vmem((2, depth, 1, Y), f32),
                vmem((2, strip, Y), f32),
                vmem((2, depth, 1, Y), f32),
                vmem((depth, strip, Y), f32),
                dma,
                dma((depth,)),
                dma((depth,)),
                dma((depth,)),
                dma,
                dma,
                dma,
                dma((depth,)),
                dma((depth,)),
                dma((depth,)),
                dma((depth,)),
                dma((2, depth)),
                dma((2, depth)),
                dma((2,)),
                dma((2,)),
            ],
            compiler_params=pltpu.CompilerParams(
                collective_id=0, has_side_effects=True, vmem_limit_bytes=60 * 1024 * 1024
            ),
        )(source, receiver, corners)

    return jax.shard_map(
        step,
        mesh=mesh,
        in_specs=(
            P(("shot", "tile"), None, None, None, None),
            P(("shot", "tile"), None, None, None, None),
            P(("shot", "tile"), None),
        ),
        out_specs=P("tile", "shot", None),
        check_vma=False,
    )
```

profile of v0, /device:TPU:1, one launch (start us, length us, event | category | flops | bytes accessed | tf_op | source)
XLA Modules:
  0.0 43.6 jit_solution(10240718609345289949)
XLA Ops:
  0.0 41.9 %shard_map.37 = f32[4,64,256]{2,1,0:T(8,128)} custom-call(bf16[2,1,32,32,128]{4,3,2,1,0:T(8,128)(2,1)} %src.1, bf16[2,1,32,32,128]{4,3,2,1,0:T(8,128)(2,1)} %rcv.1, s32[2,2]{1,0:T(2,128)} %cor.1), custom_call_target="tpu_custom_call" | custom-call | tf_op jit(solution)/shard_map/pallas_call | solution.py:340
  41.9 1.7 %copy.5 = f32[4,64,256]{2,1,0:T(8,128)} copy(f32[4,64,256]{2,1,0:T(8,128)} %shard_map.37) | data formatting | bytes 524288
where the time goes:
time: 43.7 us; the launch traced here: 43.6 us
  Pallas kernels  41.9 us (96%)
  local copies, waits for them, and re-layouts  1.67 us (4%)
    pallas_call x1, Pallas kernels, step(): pl.pallas_call(functools.partial(kernel, ns, nt), out_shape=jax.ShapeDtyp...  41.9 us
    unnamed x1, local copies, waits for them, and re-layouts  1.67 us

commit v1 on v0

v1 whole, which is shorter than its diff:
```python
import functools

import jax
import jax.numpy as jnp
from jax import lax
from jax.experimental import pallas as pl
from jax.experimental.pallas import tpu as pltpu
from jax.sharding import PartitionSpec as P

X = 256
Y = 256
LANES = 128

damping = 1.0


def partner(index, k, count):
    if count & (count - 1):
        return lax.rem(index + k, count)
    bit = 1
    result = index
    while bit < count:
        if k & bit:
            result = result + bit * (1 - 2 * lax.rem(index // bit, 2))
        bit *= 2
    return result


def plan(depth):
    if depth < 3:
        return list(range(depth)), []
    return [0, depth - 1], list(range(1, depth - 1))


def kernel(
    ns, nt, src, rcv, cor, out, sbuf, rx, cbuf, csm, boxes, acc, r1, r2, mbuf, mx, nrm, hx, hz, rows,
    in_sem, rx_send, rx_recv, c_send, c_recv, c_local,
    s1_send, s1_recv, s2_send, s2_recv, m_send, m_recv, row_send, row_recv, face_send, face_recv,
):
    depth, strip, width = nrm.shape
    spd, samples = src.shape[0], src.shape[1]
    box_rows = src.shape[3]
    halves = width // LANES
    whole, split = plan(depth)
    shots = nt * spd
    block = min(box_rows, strip)
    per_strip = strip // block
    half_ns = ns // 2
    half_nt = nt // 2
    shot = lax.axis_index("shot")
    tile = lax.axis_index("tile")
    core = lax.rem(shot, 2)
    pair = shot // 2
    other = 1 - core
    place_in_half = lax.rem(tile, half_nt)
    base = tile - place_in_half
    mirror = lax.rem(tile + half_nt, nt)

    nw, nb = len(whole), len(split)
    full = {p: n for n, p in enumerate(whole)}
    own = {p: nw + n for n, p in enumerate(split)}
    far = {p: nw + nb + n for n, p in enumerate(split)}
    units = {u: (p, nt) for p, u in full.items()}
    units.update({u: (p, half_nt) for p, u in own.items()})
    units.update({u: (p, half_nt) for p, u in far.items()})

    barrier = pltpu.get_barrier_semaphore()
    for k in range(1, ns):
        pl.semaphore_signal(barrier, inc=1, device_id={"shot": lax.rem(shot + k, ns)})
    for k in range(1, nt):
        pl.semaphore_signal(barrier, inc=1, device_id={"tile": lax.rem(tile + k, nt)})

    for w, ref in enumerate((src, rcv)):
        for i in range(spd):
            for n in range(samples):
                pltpu.make_async_copy(ref.at[i, n], sbuf.at[:, w, i, n], in_sem).start()
    pltpu.make_async_copy(cor, cbuf.at[tile], c_recv).start()
    for u, (p, count) in units.items():
        slab = mirror if u in far.values() else tile
        slot = tile if count == nt else place_in_half
        for w, ref in enumerate((src, rcv)):
            pltpu.make_async_copy(ref.at[:, :, slab * depth + p], rx.at[u, slot, w], rx_recv.at[u]).start()
    pltpu.make_async_copy(sbuf, sbuf, in_sem).wait()

    pl.semaphore_wait(barrier, ns - 1 + nt - 1)

    for k in range(nt - 1, 0, -1):
        pltpu.make_async_remote_copy(
            src_ref=cor, dst_ref=cbuf.at[tile], send_sem=c_send, recv_sem=c_recv,
            device_id={"tile": partner(tile, k, nt)},
        ).start()

    def send_near(u):
        p = units[u][0]
        for k in range(half_nt - 1, 0, -1):
            to = base + partner(place_in_half, k, half_nt)
            slab = lax.rem(to + half_nt, nt) if u in far.values() else to
            slot = tile if units[u][1] == nt else place_in_half
            pltpu.make_async_remote_copy(
                src_ref=sbuf.at[slab * depth + p], dst_ref=rx.at[u, slot],
                send_sem=rx_send.at[u], recv_sem=rx_recv.at[u], device_id={"tile": to},
            ).start()

    def send_far(u):
        p = units[u][0]
        for k in range(half_nt):
            to = (half_nt - base) + partner(place_in_half, k, half_nt)
            pltpu.make_async_remote_copy(
                src_ref=sbuf.at[to * depth + p], dst_ref=rx.at[u, tile],
                send_sem=rx_send.at[u], recv_sem=rx_recv.at[u], device_id={"tile": to},
            ).start()

    for p in split:
        send_near(far[p])
    for p in whole:
        send_far(full[p])
    for p in whole:
        send_near(full[p])
    for p in split:
        send_near(own[p])

    edges = (
        (shot < ns - 1, shot > 0, {"shot": lax.rem(shot + 1, ns)}),
        (shot > 0, shot < ns - 1, {"shot": lax.rem(shot + ns - 1, ns)}),
    )
    faces = (
        (tile < nt - 1, tile > 0, {"tile": lax.rem(tile + 1, nt)}, depth - 1),
        (tile > 0, tile < nt - 1, {"tile": lax.rem(tile + nt - 1, nt)}, 0),
    )
    for d in range(2):
        @pl.when(jnp.logical_not(edges[d][1]))
        def _(d=d):
            hx[d] = jnp.zeros((depth, 1, width), jnp.float32)

        @pl.when(jnp.logical_not(faces[d][1]))
        def _(d=d):
            hz[d] = jnp.zeros((strip, width), jnp.float32)

    def edge_copy(d, p):
        return pltpu.make_async_remote_copy(
            src_ref=rows.at[d, p], dst_ref=hx.at[d, p],
            send_sem=row_send.at[d, p], recv_sem=row_recv.at[d, p], device_id=edges[d][2],
        )

    def face_copy(d):
        return pltpu.make_async_remote_copy(
            src_ref=nrm.at[faces[d][3]], dst_ref=hz.at[d],
            send_sem=face_send.at[d], recv_sem=face_recv.at[d], device_id=faces[d][2],
        )

    def cross_copy(p):
        n = split.index(p)
        return pltpu.make_async_remote_copy(
            src_ref=mbuf.at[n], dst_ref=mx.at[n],
            send_sem=m_send.at[n], recv_sem=m_recv.at[n], device_id={"tile": mirror},
        )

    zero = jnp.zeros((block, LANES), jnp.float32)

    def clear(s, carry):
        for q in range(2):
            for h in range(halves):
                boxes[s, q, h, pl.ds(0, block), :] = zero
                boxes[s, q, h, pl.ds(block + box_rows, block), :] = zero
        return carry

    lax.fori_loop(0, shots, clear, 0)

    pltpu.make_async_copy(cbuf, cbuf, c_recv).wait()
    to_scalar = pltpu.make_async_copy(cbuf, csm, c_local)
    to_scalar.start()
    to_scalar.wait()

    lane = lax.broadcasted_iota(jnp.int32, (box_rows, LANES), 1)

    def expand(u):
        first_tile = 0 if units[u][1] == nt else base

        def peer(t, carry):
            for i in range(spd):
                s = t * spd + i
                col = csm[first_tile + t, i, 1]
                turn = lax.rem(col, LANES)
                image = jnp.zeros((box_rows, LANES), jnp.float32)
                light = image
                for n in range(samples):
                    wave = rx[u, t, 0, i, n].astype(jnp.float32)
                    back = rx[u, t, 1, i, n].astype(jnp.float32)
                    image = wave * back if n == 0 else image + wave * back
                    light = wave * wave if n == 0 else light + wave * wave
                image = pltpu.roll(image, turn, 1)
                light = pltpu.roll(light, turn, 1)
                for h in range(halves):
                    at = lane + (h * LANES - col)
                    inside = (at >= 0) & (at < LANES)
                    boxes[s, 0, h, pl.ds(block, box_rows), :] = jnp.where(inside, image, 0.0)
                    boxes[s, 1, h, pl.ds(block, box_rows), :] = jnp.where(inside, light, 0.0)
            return carry

        lax.fori_loop(0, units[u][1], peer, 0)

    def place(u, parity):
        first_tile = 0 if units[u][1] == nt else base

        def one(n, carry):
            j = 2 * (n // per_strip) + parity
            at = lax.rem(n, per_strip) * block
            first = j * strip + at + block
            total = [[None] * halves for _ in range(2)]
            for s in range(units[u][1] * spd):
                start = jnp.clip(first - csm[first_tile + s // spd, s % spd, 0], 0, box_rows + block)
                for q in range(2):
                    for h in range(halves):
                        piece = boxes[s, q, h, pl.ds(start, block), :]
                        total[q][h] = piece if s == 0 else total[q][h] + piece
            for q in range(2):
                for h in range(halves):
                    acc[u, j, q, pl.ds(at, block), pl.ds(h * LANES, LANES)] = total[q][h]
            return carry

        lax.fori_loop(0, half_ns * per_strip, one, 0)

    def stage1(u):
        for i in range(half_ns):
            pltpu.make_async_remote_copy(
                src_ref=acc.at[u, 2 * i + other],
                dst_ref=r1.at[u, i],
                send_sem=s1_send.at[u],
                recv_sem=s1_recv.at[u],
                device_id={"shot": 2 * pair + other},
            ).start()

    def gather(u):
        got = rx.at[u] if units[u][1] == nt else rx.at[u, pl.ds(0, half_nt)]
        pltpu.make_async_copy(got, got, rx_recv.at[u]).wait()
        expand(u)
        place(u, other)
        stage1(u)
        place(u, core)

    def stage2(u):
        pltpu.make_async_copy(r1.at[u], r1.at[u], s1_recv.at[u]).wait()
        for k in range(1, half_ns):
            to = lax.rem(pair + k, half_ns)
            j = 2 * to + core
            acc[u, j] = acc[u, j] + r1[u, to]
            pltpu.make_async_remote_copy(
                src_ref=acc.at[u, j],
                dst_ref=r2.at[u, k - 1],
                send_sem=s2_send.at[u],
                recv_sem=s2_recv.at[u],
                device_id={"shot": j},
            ).start()

    def totals(u):
        pltpu.make_async_copy(r2.at[u], r2.at[u], s2_recv.at[u]).wait()
        image = acc[u, shot, 0] + r1[u, pair, 0]
        light = acc[u, shot, 1] + r1[u, pair, 1]
        for k in range(half_ns - 1):
            image = image + r2[u, k, 0]
            light = light + r2[u, k, 1]
        return image, light

    def cross(p):
        n = split.index(p)
        image, light = totals(far[p])
        mbuf[n, 0] = image
        mbuf[n, 1] = light
        cross_copy(p).start()

    def finish(p):
        if p in full:
            image, light = totals(full[p])
        else:
            n = split.index(p)
            image, light = totals(own[p])
            cross_copy(p).wait_recv()
            image = image + mx[n, 0]
            light = light + mx[n, 1]
        normal = image / (damping + light)
        nrm[p] = normal
        rows[0, p] = normal[strip - 1 :, :]
        rows[1, p] = normal[:1, :]
        for d in range(2):
            @pl.when(edges[d][0])
            def _(d=d):
                edge_copy(d, p).start()

            if p == faces[d][3]:
                @pl.when(faces[d][0])
                def _(d=d):
                    face_copy(d).start()

    row = lax.broadcasted_iota(jnp.int32, (strip, width), 0)
    column = lax.broadcasted_iota(jnp.int32, (strip, width), 1)

    def lateral(p):
        center = nrm[p]
        before = jnp.where(row == 0, 0.0, pltpu.roll(center, 1, 0))
        after = jnp.where(row == strip - 1, 0.0, pltpu.roll(center, strip - 1, 0))
        left = jnp.where(column == 0, 0.0, pltpu.roll(center, 1, 1))
        right = jnp.where(column == width - 1, 0.0, pltpu.roll(center, width - 1, 1))
        return before + after + left + right - 6.0 * center

    def wait_edges(p):
        for d in range(2):
            @pl.when(edges[d][1])
            def _(d=d):
                edge_copy(d, p).wait_recv()

    def add_edges(p):
        out[p, pl.ds(0, 1), :] = out[p, pl.ds(0, 1), :] + hx[0, p]
        out[p, pl.ds(strip - 1, 1), :] = out[p, pl.ds(strip - 1, 1), :] + hx[1, p]

    def near_planes(p):
        return [q for q in (p - 1, p + 1) if 0 <= q < depth]

    def base_plane(p, known):
        value = lateral(p)
        for q in near_planes(p):
            if q in known:
                value = value + nrm[q]
        for d in range(2):
            if p == (depth - 1 if d else 0):
                @pl.when(faces[d][1])
                def _(d=d):
                    face_copy(d).wait_recv()
                value = value + hz[d]
        out[p] = value
        wait_edges(p)
        add_edges(p)

    first, last = split[0], split[-1]
    middle = split[:-1]

    for p in split:
        gather(far[p])
    for p in split:
        stage2(far[p])
    rest = [full[whole[0]]] + [own[p] for p in middle] + [full[p] for p in whole[1:]] + [own[last]]
    for n, u in enumerate(rest):
        gather(u)
        if n < nb:
            cross(split[n])
        if n >= 1 and units[rest[n - 1]][1] == nt:
            pass
        stage2(u)
    for p in whole:
        finish(p)
    for p in middle:
        finish(p)
    known = whole + middle
    for p in known:
        base_plane(p, known)
    finish(last)
    for p in near_planes(last):
        out[p] = out[p] + nrm[last]
    base_plane(last, known)

    for d in range(2):
        @pl.when(edges[d][0])
        def _(d=d):
            for p in range(depth):
                edge_copy(d, p).wait_send()

        @pl.when(faces[d][0])
        def _(d=d):
            face_copy(d).wait_send()

    sent = cbuf.at[pl.ds(0, nt - 1)]
    pltpu.make_async_copy(sent, sent, c_send).wait()
    for u, (p, count) in units.items():
        sent = rx.at[u, pl.ds(0, count - 1)]
        pltpu.make_async_copy(sent, sent, rx_send.at[u]).wait()
        pltpu.make_async_copy(r1.at[u], r1.at[u], s1_send.at[u]).wait()
        pltpu.make_async_copy(r2.at[u], r2.at[u], s2_send.at[u]).wait()
    for p in split:
        cross_copy(p).wait_send()


def solution(mesh):
    ns, nt = mesh.shape["shot"], mesh.shape["tile"]

    def step(source, receiver, corners):
        spd, samples, full_depth, box_rows, box_cols = source.shape
        depth = full_depth // nt
        strip = X // ns
        block = min(box_rows, strip)
        half_ns = ns // 2
        whole, split = plan(depth)
        nb = len(split)
        count = len(whole) + 2 * nb
        vmem = pltpu.VMEM
        dma = pltpu.SemaphoreType.DMA
        f32 = jnp.float32
        return pl.pallas_call(
            functools.partial(kernel, ns, nt),
            out_shape=jax.ShapeDtypeStruct((depth, strip, Y), f32),
            in_specs=[pl.BlockSpec(memory_space=pl.ANY)] * 3,
            out_specs=pl.BlockSpec(memory_space=pltpu.VMEM),
            scratch_shapes=[
                vmem((full_depth, 2, spd, samples, box_rows, box_cols), jnp.bfloat16),
                vmem((count, nt, 2, spd, samples, box_rows, box_cols), jnp.bfloat16),
                vmem((nt, spd, 2), jnp.int32),
                pltpu.SMEM((nt, spd, 2), jnp.int32),
                vmem((nt * spd, 2, Y // LANES, box_rows + 2 * block, LANES), f32),
                vmem((count, ns, 2, strip, Y), f32),
                vmem((count, half_ns, 2, strip, Y), f32),
                vmem((count, half_ns - 1, 2, strip, Y), f32),
                vmem((max(nb, 1), 2, strip, Y), f32),
                vmem((max(nb, 1), 2, strip, Y), f32),
                vmem((depth, strip, Y), f32),
                vmem((2, depth, 1, Y), f32),
                vmem((2, strip, Y), f32),
                vmem((2, depth, 1, Y), f32),
                dma,
                dma((count,)),
                dma((count,)),
                dma,
                dma,
                dma,
                dma((count,)),
                dma((count,)),
                dma((count,)),
                dma((count,)),
                dma((max(nb, 1),)),
                dma((max(nb, 1),)),
                dma((2, depth)),
                dma((2, depth)),
                dma((2,)),
                dma((2,)),
            ],
            compiler_params=pltpu.CompilerParams(
                collective_id=0, has_side_effects=True, vmem_limit_bytes=54700 * 1024
            ),
        )(source, receiver, corners)

    return jax.shard_map(
        step,
        mesh=mesh,
        in_specs=(
            P(("shot", "tile"), None, None, None, None),
            P(("shot", "tile"), None, None, None, None),
            P(("shot", "tile"), None),
        ),
        out_specs=P("tile", "shot", None),
        check_vma=False,
    )
```

time: 43.7 us -> 37.9 us (0.87)
  Pallas kernels: 41.9 us -> 36.3 us
    pallas_call x1, Pallas kernels: 41.9 us -> 36.3 us  [step(): pl.pallas_call(functools.partial(kernel, ns, nt), out_shape=jax.ShapeDtyp...]
    unnamed x1 -> x3, local copies, waits for them, and re-layouts: 1.67 us -> 1.38 us
where the time goes in v1:
time: 37.9 us; the launch traced here: 37.7 us
  Pallas kernels  36.3 us (96%)
  local copies, waits for them, and re-layouts  1.38 us (4%)
    pallas_call x1, Pallas kernels, step(): pl.pallas_call(functools.partial(kernel, ns, nt), out_shape=jax.ShapeDtyp...  36.3 us
    unnamed x3, local copies, waits for them, and re-layouts  1.38 us

profile of v1, /device:TPU:1, one launch (start us, length us, event | category | flops | bytes accessed | tf_op | source)
XLA Modules:
  0.0 37.7 jit_solution(15087638975791009436)
XLA Ops:
  0.0 0.0 copy-start
  0.0 0.7 %copy-done = s32[2,2]{1,0:T(2,128)S(1)} copy-done((s32[2,2]{1,0:T(2,128)S(1)}, s32[2,2]{1,0:T(2,128)}, u32[]{:S(2)}) %copy-start) | copy-done | bytes 40
  0.7 36.3 %shard_map.37 = f32[4,64,256]{2,1,0:T(8,128)S(1)} custom-call(bf16[2,1,32,32,128]{4,3,2,1,0:T(8,128)(2,1)} %src.1, bf16[2,1,32,32,128]{4,3,2,1,0:T(8,128)(2,1)} %rcv.1, s32[2,2]{1,0:T(2,128)S(1)} %copy-done), custom_call_target="tpu_custom_call" | custom-call | tf_op jit(solution)/shard_map/pallas_call | solution.py:396
  37.0 0.7 %copy.5 = f32[4,64,256]{2,1,0:T(8,128)} copy(f32[4,64,256]{2,1,0:T(8,128)S(1)} %shard_map.37) | data formatting | bytes 524288
Async XLA Ops:
  0.0 0.7 %copy-start = (s32[2,2]{1,0:T(2,128)S(1)}, s32[2,2]{1,0:T(2,128)}, u32[]{:S(2)}) copy-start(s32[2,2]{1,0:T(2,128)} %cor.1) | copy-start | bytes 52

commit v2 on v1

v2 whole, which is shorter than its diff:
```python
import functools

import jax
import jax.numpy as jnp
from jax import lax
from jax.experimental import pallas as pl
from jax.experimental.pallas import tpu as pltpu
from jax.sharding import PartitionSpec as P

X = 256
Y = 256
LANES = 128

damping = 1.0


def partner(index, k, count):
    if count & (count - 1):
        return lax.rem(index + k, count)
    bit = 1
    result = index
    while bit < count:
        if k & bit:
            result = result + bit * (1 - 2 * lax.rem(index // bit, 2))
        bit *= 2
    return result


def partner_back(index, k, count):
    if count & (count - 1):
        return lax.rem(index + count - k, count)
    return partner(index, k, count)


def plan(depth):
    if depth < 3:
        return list(range(depth)), []
    return [0, depth - 1], list(range(1, depth - 1))


def kernel(
    ns, nt, src, rcv, cor, out, sbuf, rxw, rxh, cbuf, csm, cby, csy, boxes,
    acc, r1, r2, hacc, hr1, hal, hal1, mbuf, mx, mhal, mhx, nrm, hx, hz, rows,
    in_sem, rxw_send, rxw_recv, rxh_send, rxh_recv, ry_send, ry_recv,
    c_send, c_recv, cn_send, cn_recv, cy_send, cy_recv, c_local,
    s1_send, s1_recv, s2_send, s2_recv, h1_send, h1_recv, m_send, m_recv,
    row_send, row_recv, face_send, face_recv, known_sem,
):
    depth, strip, width = nrm.shape
    spd, samples = src.shape[0], src.shape[1]
    box_rows = src.shape[3]
    halves = width // LANES
    whole, split = plan(depth)
    block = min(box_rows, strip)
    per_strip = strip // block
    half_ns = ns // 2
    half_nt = nt // 2
    shot = lax.axis_index("shot")
    tile = lax.axis_index("tile")
    core = lax.rem(shot, 2)
    pair = shot // 2
    other = 1 - core
    mine = lax.rem(tile, half_nt)
    base = tile - mine
    mirror = lax.rem(tile + half_nt, nt)
    twin = {"shot": 2 * pair + other}
    nb = len(split)
    far = range(nb)
    own = range(nb, 2 * nb)
    plane = split + split

    def peer_shot(m):
        return {"shot": 2 * lax.rem(pair + m, half_ns) + core}

    def slab_of(u, to):
        return lax.rem(to + half_nt, nt) if u in far else to

    barrier = pltpu.get_barrier_semaphore()
    for k in range(1, ns):
        pl.semaphore_signal(barrier, inc=1, device_id={"shot": lax.rem(shot + k, ns)})
    column, side = tile // 2, lax.rem(tile, 2)
    columns = nt // 2
    around = (
        (None, {"tile": tile + 1 - 2 * side}),
        (column > 0, {"tile": lax.rem(tile + nt - 2, nt)}),
        (column < columns - 1, {"tile": lax.rem(tile + 2, nt)}),
    )

    def greet(sem):
        for there, who in around:
            if there is None:
                pl.semaphore_signal(sem, inc=1, device_id=who)
            else:
                @pl.when(there)
                def _(who=who):
                    pl.semaphore_signal(sem, inc=1, device_id=who)

    def await_greetings(sem, more):
        pl.semaphore_wait(sem, more + 1 + jnp.minimum(column, 1) + jnp.minimum(columns - 1 - column, 1))

    def learn(r):
        await_greetings(known_sem.at[r], 0)
        if r + 1 < known_sem.shape[0]:
            greet(known_sem.at[r + 1])

    greet(barrier)

    for w, ref in enumerate((src, rcv)):
        for i in range(spd):
            for n in range(samples):
                pltpu.make_async_copy(ref.at[i, n], sbuf.at[:, w, i, n], in_sem).start()
    pltpu.make_async_copy(cor, cbuf.at[tile], c_recv).start()
    pltpu.make_async_copy(cor, cby.at[0, mine], cn_recv).start()
    for w, ref in enumerate((src, rcv)):
        for u, p in enumerate(plane):
            pltpu.make_async_copy(
                ref.at[:, :, slab_of(u, tile) * depth + p], rxh.at[u, 0, mine, w], rxh_recv.at[u, 0]
            ).start()
        for u, p in enumerate(whole):
            pltpu.make_async_copy(ref.at[:, :, tile * depth + p], rxw.at[u, tile, w], rxw_recv.at[u]).start()
    pltpu.make_async_copy(sbuf, sbuf, in_sem).wait()

    await_greetings(barrier, ns - 1)
    greet(known_sem.at[0])

    def remote(src_ref, dst_ref, send_sem, recv_sem, device_id):
        pltpu.make_async_remote_copy(
            src_ref=src_ref, dst_ref=dst_ref, send_sem=send_sem, recv_sem=recv_sem, device_id=device_id
        ).start()

    def steps(to):
        return abs(to // 2 - column) + abs(lax.rem(to, 2) - side)

    def near_half(u, when=None):
        for k in range(1, half_nt):
            to = base + partner(mine, k, half_nt)
            guarded(when, to, lambda k=k, to=to: remote(
                sbuf.at[slab_of(u, to) * depth + plane[u]], rxh.at[u, 0, mine],
                rxh_send.at[u], rxh_recv.at[u, k], {"tile": to},
            ))

    def guarded(when, to, send):
        if when is None:
            send()
        else:
            @pl.when(when(steps(to)))
            def _():
                send()

    def own_half(u):
        for m in range(1, half_ns):
            remote(
                sbuf.at[slab_of(u, tile) * depth + plane[u]], rxh.at[u, m, mine],
                ry_send.at[u], ry_recv.at[u], peer_shot(m),
            )

    def relay(u):
        for k in range(1, half_nt):
            slot = partner_back(mine, k, half_nt)
            got = rxh.at[u, 0, slot]
            pltpu.make_async_copy(got, got, rxh_recv.at[u, k]).wait()
            for m in range(1, half_ns):
                remote(got, rxh.at[u, m, slot], ry_send.at[u], ry_recv.at[u], peer_shot(m))

    def near_whole(u, when=None):
        for k in range(1, half_nt):
            to = base + partner(mine, k, half_nt)
            guarded(when, to, lambda to=to: remote(
                sbuf.at[to * depth + whole[u]], rxw.at[u, tile], rxw_send.at[u], rxw_recv.at[u], {"tile": to}
            ))

    def far_whole(u, when=None):
        for k in range(half_nt):
            to = (half_nt - base) + partner(mine, k, half_nt)
            guarded(when, to, lambda to=to: remote(
                sbuf.at[to * depth + whole[u]], rxw.at[u, tile], rxw_send.at[u], rxw_recv.at[u], {"tile": to}
            ))

    def corners(when):
        for k in range(1, half_nt):
            to = base + partner(mine, k, half_nt)
            guarded(when, to, lambda to=to: remote(cor, cby.at[0, mine], cn_send, cn_recv, {"tile": to}))
        for k in range(1, nt):
            to = partner(tile, k, nt)
            guarded(when, to, lambda to=to: remote(cor, cbuf.at[tile], c_send, c_recv, {"tile": to}))

    for level in (1, 2, 3):
        if level == 1:
            when = lambda d: d == 1
        elif level == 2:
            learn(0)
            when = lambda d: d == 2
        else:
            for r in range(1, known_sem.shape[0]):
                learn(r)
            when = lambda d: d > 2
        corners(when)
        near_half(far[0], when)
        far_whole(0, when)
        if level == 1:
            for u in range(2 * nb):
                own_half(u)
    for u in far[1:]:
        near_half(u)
    near_whole(0)
    near_half(own[0])
    far_whole(1)
    near_whole(1)
    for u in own[1:]:
        near_half(u)

    edges = (
        (shot < ns - 1, shot > 0, {"shot": lax.rem(shot + 1, ns)}),
        (shot > 0, shot < ns - 1, {"shot": lax.rem(shot + ns - 1, ns)}),
    )
    faces = (
        (tile < nt - 1, tile > 0, {"tile": lax.rem(tile + 1, nt)}, depth - 1),
        (tile > 0, tile < nt - 1, {"tile": lax.rem(tile + nt - 1, nt)}, 0),
    )
    for d in range(2):
        @pl.when(jnp.logical_not(edges[d][1]))
        def _(d=d):
            hx[d] = jnp.zeros((depth, 1, width), jnp.float32)

        @pl.when(jnp.logical_not(faces[d][1]))
        def _(d=d):
            hz[d] = jnp.zeros((strip, width), jnp.float32)

    def edge_copy(d, p):
        return pltpu.make_async_remote_copy(
            src_ref=rows.at[d, p], dst_ref=hx.at[d, p],
            send_sem=row_send.at[d, p], recv_sem=row_recv.at[d, p], device_id=edges[d][2],
        )

    def face_copy(d):
        return pltpu.make_async_remote_copy(
            src_ref=nrm.at[faces[d][3]], dst_ref=hz.at[d],
            send_sem=face_send.at[d], recv_sem=face_recv.at[d], device_id=faces[d][2],
        )

    def cross_copies(n):
        pieces = []
        for g, (a, b) in enumerate(((mbuf, mx), (mhal, mhx))):
            pieces.append(pltpu.make_async_remote_copy(
                src_ref=a.at[n], dst_ref=b.at[n],
                send_sem=m_send.at[n, g], recv_sem=m_recv.at[n, g], device_id={"tile": mirror},
            ))
        return pieces

    zero = jnp.zeros((block, LANES), jnp.float32)

    def clear(s, carry):
        for q in range(2):
            for h in range(halves):
                boxes[s, q, h, pl.ds(0, block), :] = zero
                boxes[s, q, h, pl.ds(block + box_rows, block), :] = zero
        return carry

    lax.fori_loop(0, boxes.shape[0], clear, 0)

    lane = lax.broadcasted_iota(jnp.int32, (box_rows, LANES), 1)

    def expand_one(s, col, wave_of, back_of):
        turn = lax.rem(col, LANES)
        image = jnp.zeros((box_rows, LANES), jnp.float32)
        light = image
        for n in range(samples):
            wave = wave_of(n).astype(jnp.float32)
            back = back_of(n).astype(jnp.float32)
            image = wave * back if n == 0 else image + wave * back
            light = wave * wave if n == 0 else light + wave * wave
        image = pltpu.roll(image, turn, 1)
        light = pltpu.roll(light, turn, 1)
        for h in range(halves):
            at = lane + (h * LANES - col)
            inside = (at >= 0) & (at < LANES)
            boxes[s, 0, h, pl.ds(block, box_rows), :] = jnp.where(inside, image, 0.0)
            boxes[s, 1, h, pl.ds(block, box_rows), :] = jnp.where(inside, light, 0.0)

    def expand_whole(u):
        def peer(t, carry):
            for i in range(spd):
                expand_one(
                    t * spd + i, csm[t, i, 1],
                    lambda n: rxw[u, t, 0, i, n], lambda n: rxw[u, t, 1, i, n],
                )
            return carry

        lax.fori_loop(0, nt, peer, 0)

    def expand_half(u):
        for m in range(half_ns):
            def peer(t, carry):
                for i in range(spd):
                    expand_one(
                        (m * half_nt + t) * spd + i, csy[m, t, i, 1],
                        lambda n: rxh[u, m, t, 0, i, n], lambda n: rxh[u, m, t, 1, i, n],
                    )
                return carry

            lax.fori_loop(0, half_nt, peer, 0)

    whole_rows = [(s, lambda s=s: csm[s // spd, s % spd, 0]) for s in range(nt * spd)]
    half_rows = [
        ((m * half_nt + t) * spd + i, lambda m=m, t=t, i=i: csy[m, t, i, 0])
        for m in range(half_ns) for t in range(half_nt) for i in range(spd)
    ]

    def stack(corner_rows, first, count):
        total = [[None] * halves for _ in range(2)]
        for s, corner in corner_rows:
            start = jnp.clip(first + block - corner(), 0, box_rows + block)
            for q in range(2):
                for h in range(halves):
                    piece = boxes[s, q, h, pl.ds(start, count), :]
                    total[q][h] = piece if total[q][h] is None else total[q][h] + piece
        return total

    def place_whole(u, parity):
        def one(n, carry):
            j = 2 * (n // per_strip) + parity
            at = lax.rem(n, per_strip) * block
            total = stack(whole_rows, j * strip + at, block)
            for q in range(2):
                for h in range(halves):
                    acc[u, j, q, pl.ds(at, block), pl.ds(h * LANES, LANES)] = total[q][h]
            return carry

        lax.fori_loop(0, half_ns * per_strip, one, 0)

    def place_half(u, parity):
        top = (2 * pair + parity) * strip

        def one(n, carry):
            at = n * block
            total = stack(half_rows, top + at, block)
            for q in range(2):
                for h in range(halves):
                    hacc[u, parity, q, pl.ds(at, block), pl.ds(h * LANES, LANES)] = total[q][h]
            return carry

        lax.fori_loop(0, per_strip, one, 0)
        for d, first in enumerate((top - 1, top + strip)):
            total = stack(half_rows, first, 1)
            for q in range(2):
                for h in range(halves):
                    hal[u, parity, pl.ds(2 * q + d, 1), pl.ds(h * LANES, LANES)] = total[q][h]

    def gather_whole(u):
        pltpu.make_async_copy(rxw.at[u], rxw.at[u], rxw_recv.at[u]).wait()
        expand_whole(u)
        place_whole(u, other)
        for i in range(half_ns):
            remote(acc.at[u, 2 * i + other], r1.at[u, i], s1_send.at[u], s1_recv.at[u], twin)
        place_whole(u, core)

    def gather_half(u):
        got = rxh.at[u, 0, mine]
        pltpu.make_async_copy(got, got, rxh_recv.at[u, 0]).wait()
        got = rxh.at[u, pl.ds(1, half_ns - 1)]
        pltpu.make_async_copy(got, got, ry_recv.at[u]).wait()
        expand_half(u)
        place_half(u, other)
        remote(hacc.at[u, other], hr1.at[u], h1_send.at[u, 0], h1_recv.at[u, 0], twin)
        remote(hal.at[u, other], hal1.at[u], h1_send.at[u, 1], h1_recv.at[u, 1], twin)
        place_half(u, core)

    def wait_twin(u):
        pltpu.make_async_copy(hr1.at[u], hr1.at[u], h1_recv.at[u, 0]).wait()
        pltpu.make_async_copy(hal1.at[u], hal1.at[u], h1_recv.at[u, 1]).wait()

    def stage2(u):
        pltpu.make_async_copy(r1.at[u], r1.at[u], s1_recv.at[u]).wait()
        for k in range(1, half_ns):
            to = lax.rem(pair + k, half_ns)
            j = 2 * to + core
            acc[u, j] = acc[u, j] + r1[u, to]
            remote(acc.at[u, j], r2.at[u, k - 1], s2_send.at[u], s2_recv.at[u], {"shot": j})

    def cross(n):
        u = far[n]
        wait_twin(u)
        mhal[n] = hal[u, core] + hal1[u]
        mbuf[n] = hacc[u, core] + hr1[u]
        for copy in reversed(cross_copies(n)):
            copy.start()

    def finish_whole(u):
        p = whole[u]
        pltpu.make_async_copy(r2.at[u], r2.at[u], s2_recv.at[u]).wait()
        image = acc[u, shot, 0] + r1[u, pair, 0]
        light = acc[u, shot, 1] + r1[u, pair, 1]
        for k in range(half_ns - 1):
            image = image + r2[u, k, 0]
            light = light + r2[u, k, 1]
        normal = image / (damping + light)
        nrm[p] = normal
        rows[0, p] = normal[strip - 1 :, :]
        rows[1, p] = normal[:1, :]
        for d in range(2):
            @pl.when(edges[d][0])
            def _(d=d):
                edge_copy(d, p).start()

            if p == faces[d][3]:
                @pl.when(faces[d][0])
                def _(d=d):
                    face_copy(d).start()

    def finish_half(n):
        p, u = split[n], own[n]
        wait_twin(u)
        for copy in cross_copies(n):
            copy.wait_recv()
        image = (hacc[u, core, 0] + hr1[u, 0]) + mx[n, 0]
        light = (hacc[u, core, 1] + hr1[u, 1]) + mx[n, 1]
        nrm[p] = image / (damping + light)
        rim = hal[u, core] + hal1[u] + mhx[n]
        rim = rim[0:2, :] / (damping + rim[2:4, :])
        hx[0, p] = rim[0:1, :]
        hx[1, p] = rim[1:2, :]

    row = lax.broadcasted_iota(jnp.int32, (strip, width), 0)
    lanes = lax.broadcasted_iota(jnp.int32, (strip, width), 1)

    def lateral(p):
        center = nrm[p]
        before = jnp.where(row == 0, hx[0, p], pltpu.roll(center, 1, 0))
        after = jnp.where(row == strip - 1, hx[1, p], pltpu.roll(center, strip - 1, 0))
        left = jnp.where(lanes == 0, 0.0, pltpu.roll(center, 1, 1))
        right = jnp.where(lanes == width - 1, 0.0, pltpu.roll(center, width - 1, 1))
        return before + after + left + right - 6.0 * center

    def near_planes(p):
        return [q for q in (p - 1, p + 1) if 0 <= q < depth]

    def base_plane(p, known):
        if p in whole:
            for d in range(2):
                @pl.when(edges[d][1])
                def _(d=d):
                    edge_copy(d, p).wait_recv()
        value = lateral(p)
        for q in near_planes(p):
            if q in known:
                value = value + nrm[q]
        for d in range(2):
            if p == (depth - 1 if d else 0):
                @pl.when(faces[d][1])
                def _(d=d):
                    face_copy(d).wait_recv()
                value = value + hz[d]
        out[p] = value

    last = split[-1]
    middle = split[:-1]

    pltpu.make_async_copy(cby.at[0], cby.at[0], cn_recv).wait()
    for m in range(1, half_ns):
        remote(cby.at[0], cby.at[m], cy_send, cy_recv, peer_shot(m))
    relay(far[0])
    peers = cby.at[pl.ds(1, half_ns - 1)]
    pltpu.make_async_copy(peers, peers, cy_recv).wait()
    half_corners = pltpu.make_async_copy(cby, csy, c_local.at[0])
    half_corners.start()
    pltpu.make_async_copy(cbuf, cbuf, c_recv).wait()
    all_corners = pltpu.make_async_copy(cbuf, csm, c_local.at[1])
    all_corners.start()
    half_corners.wait()
    all_corners.wait()

    gather_half(far[0])
    for u in far[1:]:
        relay(u)
    gather_whole(0)
    cross(0)
    stage2(0)
    for n in range(1, nb):
        gather_half(far[n])
    relay(own[0])
    gather_whole(1)
    for n in range(1, nb):
        cross(n)
    for u in own[1:]:
        relay(u)
    stage2(1)
    finish_whole(0)
    for u in own[:-1]:
        gather_half(u)
    finish_whole(1)
    gather_half(own[nb - 1])
    for n in range(nb - 1):
        finish_half(n)
    known = whole + middle
    for p in known:
        base_plane(p, known)
    finish_half(nb - 1)
    for p in near_planes(last):
        out[p] = out[p] + nrm[last]
    base_plane(last, known)

    for d in range(2):
        @pl.when(edges[d][0])
        def _(d=d):
            for p in whole:
                edge_copy(d, p).wait_send()

        @pl.when(faces[d][0])
        def _(d=d):
            face_copy(d).wait_send()

    def drain(ref, sem):
        pltpu.make_async_copy(ref, ref, sem).wait()

    drain(cbuf.at[pl.ds(0, nt - 1)], c_send)
    drain(cby.at[0, pl.ds(0, half_nt - 1)], cn_send)
    drain(cby.at[pl.ds(1, half_ns - 1)], cy_send)
    for u in range(len(whole)):
        drain(rxw.at[u, pl.ds(0, nt - 1)], rxw_send.at[u])
        drain(r1.at[u], s1_send.at[u])
        drain(r2.at[u], s2_send.at[u])
    for u in range(2 * nb):
        drain(rxh.at[u, 0, pl.ds(0, half_nt - 1)], rxh_send.at[u])
        drain(rxh.at[u, pl.ds(1, half_ns - 1)], ry_send.at[u])
        drain(hr1.at[u], h1_send.at[u, 0])
        drain(hal1.at[u], h1_send.at[u, 1])
    for n in range(nb):
        for copy in cross_copies(n):
            copy.wait_send()


def solution(mesh):
    ns, nt = mesh.shape["shot"], mesh.shape["tile"]

    def step(source, receiver, corners):
        spd, samples, full_depth, box_rows, box_cols = source.shape
        depth = full_depth // nt
        strip = X // ns
        block = min(box_rows, strip)
        half_ns = ns // 2
        half_nt = nt // 2
        whole, split = plan(depth)
        nw, nb = len(whole), len(split)
        vmem = pltpu.VMEM
        dma = pltpu.SemaphoreType.DMA
        f32 = jnp.float32
        bf16 = jnp.bfloat16
        waves = (2, spd, samples, box_rows, box_cols)
        return pl.pallas_call(
            functools.partial(kernel, ns, nt),
            out_shape=jax.ShapeDtypeStruct((depth, strip, Y), f32),
            in_specs=[pl.BlockSpec(memory_space=pl.ANY)] * 3,
            out_specs=pl.BlockSpec(memory_space=pltpu.VMEM),
            scratch_shapes=[
                vmem((full_depth, *waves), bf16),
                vmem((nw, nt, *waves), bf16),
                vmem((2 * nb, half_ns, half_nt, *waves), bf16),
                vmem((nt, spd, 2), jnp.int32),
                pltpu.SMEM((nt, spd, 2), jnp.int32),
                vmem((half_ns, half_nt, spd, 2), jnp.int32),
                pltpu.SMEM((half_ns, half_nt, spd, 2), jnp.int32),
                vmem((max(nt, half_ns * half_nt) * spd, 2, Y // LANES, box_rows + 2 * block, LANES), f32),
                vmem((nw, ns, 2, strip, Y), f32),
                vmem((nw, half_ns, 2, strip, Y), f32),
                vmem((nw, half_ns - 1, 2, strip, Y), f32),
                vmem((2 * nb, 2, 2, strip, Y), f32),
                vmem((2 * nb, 2, strip, Y), f32),
                vmem((2 * nb, 2, 4, Y), f32),
                vmem((2 * nb, 4, Y), f32),
                vmem((nb, 2, strip, Y), f32),
                vmem((nb, 2, strip, Y), f32),
                vmem((nb, 4, Y), f32),
                vmem((nb, 4, Y), f32),
                vmem((depth, strip, Y), f32),
                vmem((2, depth, 1, Y), f32),
                vmem((2, strip, Y), f32),
                vmem((2, depth, 1, Y), f32),
                dma,
                dma((nw,)),
                dma((nw,)),
                dma((2 * nb,)),
                dma((2 * nb, half_nt)),
                dma((2 * nb,)),
                dma((2 * nb,)),
                dma,
                dma,
                dma,
                dma,
                dma,
                dma,
                dma((2,)),
                dma((nw,)),
                dma((nw,)),
                dma((nw,)),
                dma((nw,)),
                dma((2 * nb, 2)),
                dma((2 * nb, 2)),
                dma((nb, 2)),
                dma((nb, 2)),
                dma((2, depth)),
                dma((2, depth)),
                dma((2,)),
                dma((2,)),
                pltpu.SemaphoreType.REGULAR((nt // 2 - 1,)),
            ],
            compiler_params=pltpu.CompilerParams(
                collective_id=0, has_side_effects=True, vmem_limit_bytes=54700 * 1024
            ),
        )(source, receiver, corners)

    return jax.shard_map(
        step,
        mesh=mesh,
        in_specs=(
            P(("shot", "tile"), None, None, None, None),
            P(("shot", "tile"), None, None, None, None),
            P(("shot", "tile"), None),
        ),
        out_specs=P("tile", "shot", None),
        check_vma=False,
    )
```

time: 37.9 us -> 36.5 us (0.963)
  Pallas kernels: 36.3 us -> 34.9 us
    pallas_call x1, Pallas kernels: 36.3 us -> 34.9 us  [step(): pl.pallas_call(functools.partial(kernel, ns, nt), out_shape=jax.ShapeDtyp...]
where the time goes in v2:
time: 36.5 us; the launch traced here: 36.3 us
  Pallas kernels  34.9 us (96%)
  local copies, waits for them, and re-layouts  1.38 us (4%)
    pallas_call x1, Pallas kernels, step(): pl.pallas_call(functools.partial(kernel, ns, nt), out_shape=jax.ShapeDtyp...  34.9 us
    unnamed x3, local copies, waits for them, and re-layouts  1.38 us

profile of v2, /device:TPU:1, one launch (start us, length us, event | category | flops | bytes accessed | tf_op | source)
XLA Modules:
  0.0 36.3 jit_solution(8925914374339233955)
XLA Ops:
  0.0 0.0 copy-start
  0.0 0.7 %copy-done = s32[2,2]{1,0:T(2,128)S(1)} copy-done((s32[2,2]{1,0:T(2,128)S(1)}, s32[2,2]{1,0:T(2,128)}, u32[]{:S(2)}) %copy-start) | copy-done | bytes 40
  0.7 34.9 %shard_map.37 = f32[4,64,256]{2,1,0:T(8,128)S(1)} custom-call(bf16[2,1,32,32,128]{4,3,2,1,0:T(8,128)(2,1)} %src.1, bf16[2,1,32,32,128]{4,3,2,1,0:T(8,128)(2,1)} %rcv.1, s32[2,2]{1,0:T(2,128)S(1)} %copy-done), custom_call_target="tpu_custom_call" | custom-call | tf_op jit(solution)/shard_map/pallas_call | solution.py:549
  35.6 0.7 %copy.5 = f32[4,64,256]{2,1,0:T(8,128)} copy(f32[4,64,256]{2,1,0:T(8,128)S(1)} %shard_map.37) | data formatting | bytes 524288
Async XLA Ops:
  0.0 0.7 %copy-start = (s32[2,2]{1,0:T(2,128)S(1)}, s32[2,2]{1,0:T(2,128)}, u32[]{:S(2)}) copy-start(s32[2,2]{1,0:T(2,128)} %cor.1) | copy-start | bytes 52

commit v3 on v2

--- a/solution.py
+++ b/solution.py
@@ -131,8 +131,8 @@
     def steps(to):
         return abs(to // 2 - column) + abs(lax.rem(to, 2) - side)
 
-    def near_half(u, when=None):
-        for k in range(1, half_nt):
+    def near_half(u, when=None, first=1, stop=half_nt):
+        for k in range(first, stop):
             to = base + partner(mine, k, half_nt)
             guarded(when, to, lambda k=k, to=to: remote(
                 sbuf.at[slab_of(u, to) * depth + plane[u]], rxh.at[u, 0, mine],
@@ -154,8 +154,8 @@
                 ry_send.at[u], ry_recv.at[u], peer_shot(m),
             )
 
-    def relay(u):
-        for k in range(1, half_nt):
+    def relay(u, first=1, stop=half_nt):
+        for k in range(first, stop):
             slot = partner_back(mine, k, half_nt)
             got = rxh.at[u, 0, slot]
             pltpu.make_async_copy(got, got, rxh_recv.at[u, k]).wait()
@@ -200,14 +200,15 @@
         if level == 1:
             for u in range(2 * nb):
                 own_half(u)
+            for u in own:
+                near_half(u, None, 1, 2)
+        near_whole(0, when)
     for u in far[1:]:
         near_half(u)
-    near_whole(0)
-    near_half(own[0])
     far_whole(1)
     near_whole(1)
-    for u in own[1:]:
-        near_half(u)
+    for u in own:
+        near_half(u, None, 2)
 
     edges = (
         (shot < ns - 1, shot > 0, {"shot": lax.rem(shot + 1, ns)}),
@@ -288,8 +289,8 @@
 
         lax.fori_loop(0, nt, peer, 0)
 
-    def expand_half(u):
-        for m in range(half_ns):
+    def expand_half(u, first, stop):
+        for m in range(first, stop):
             def peer(t, carry):
                 for i in range(spd):
                     expand_one(
@@ -357,9 +358,10 @@
     def gather_half(u):
         got = rxh.at[u, 0, mine]
         pltpu.make_async_copy(got, got, rxh_recv.at[u, 0]).wait()
+        expand_half(u, 0, 1)
         got = rxh.at[u, pl.ds(1, half_ns - 1)]
         pltpu.make_async_copy(got, got, ry_recv.at[u]).wait()
-        expand_half(u)
+        expand_half(u, 1, half_ns)
         place_half(u, other)
         remote(hacc.at[u, other], hr1.at[u], h1_send.at[u, 0], h1_recv.at[u, 0], twin)
         remote(hal.at[u, other], hal1.at[u], h1_send.at[u, 1], h1_recv.at[u, 1], twin)
@@ -463,27 +465,28 @@
     pltpu.make_async_copy(peers, peers, cy_recv).wait()
     half_corners = pltpu.make_async_copy(cby, csy, c_local.at[0])
     half_corners.start()
+    for u in own:
+        relay(u, 1, 2)
+    half_corners.wait()
+
+    gather_half(far[0])
     pltpu.make_async_copy(cbuf, cbuf, c_recv).wait()
     all_corners = pltpu.make_async_copy(cbuf, csm, c_local.at[1])
     all_corners.start()
-    half_corners.wait()
-    all_corners.wait()
-
-    gather_half(far[0])
     for u in far[1:]:
         relay(u)
+    all_corners.wait()
     gather_whole(0)
     cross(0)
     stage2(0)
     for n in range(1, nb):
         gather_half(far[n])
-    relay(own[0])
+        cross(n)
     gather_whole(1)
-    for n in range(1, nb):
-        cross(n)
+    relay(own[0], 2)
+    stage2(1)
     for u in own[1:]:
-        relay(u)
-    stage2(1)
+        relay(u, 2)
     finish_whole(0)
     for u in own[:-1]:
         gather_half(u)

time: 36.5 us -> 33.1 us (0.907)
  Pallas kernels: 34.9 us -> 31.5 us
    pallas_call x1, Pallas kernels: 34.9 us -> 31.5 us  [step(): pl.pallas_call(functools.partial(kernel, ns, nt), out_shape=jax.ShapeDtyp...]
where the time goes in v3:
time: 33.1 us; the launch traced here: 32.9 us
  Pallas kernels  31.5 us (95%)
  local copies, waits for them, and re-layouts  1.38 us (4%)
    pallas_call x1, Pallas kernels, step(): pl.pallas_call(functools.partial(kernel, ns, nt), out_shape=jax.ShapeDtyp...  31.5 us
    unnamed x3, local copies, waits for them, and re-layouts  1.38 us

profile of v3, /device:TPU:1, one launch (start us, length us, event | category | flops | bytes accessed | tf_op | source)
XLA Modules:
  0.0 32.9 jit_solution(2959869711523057073)
XLA Ops:
  0.0 0.0 copy-start
  0.0 0.7 %copy-done = s32[2,2]{1,0:T(2,128)S(1)} copy-done((s32[2,2]{1,0:T(2,128)S(1)}, s32[2,2]{1,0:T(2,128)}, u32[]{:S(2)}) %copy-start) | copy-done | bytes 40
  0.7 31.5 %shard_map.37 = f32[4,64,256]{2,1,0:T(8,128)S(1)} custom-call(bf16[2,1,32,32,128]{4,3,2,1,0:T(8,128)(2,1)} %src.1, bf16[2,1,32,32,128]{4,3,2,1,0:T(8,128)(2,1)} %rcv.1, s32[2,2]{1,0:T(2,128)S(1)} %copy-done), custom_call_target="tpu_custom_call" | custom-call | tf_op jit(solution)/shard_map/pallas_call | solution.py:552
  32.2 0.7 %copy.5 = f32[4,64,256]{2,1,0:T(8,128)} copy(f32[4,64,256]{2,1,0:T(8,128)S(1)} %shard_map.37) | data formatting | bytes 524288
Async XLA Ops:
  0.0 0.7 %copy-start = (s32[2,2]{1,0:T(2,128)S(1)}, s32[2,2]{1,0:T(2,128)}, u32[]{:S(2)}) copy-start(s32[2,2]{1,0:T(2,128)} %cor.1) | copy-start | bytes 52

commit v4 on v3

--- a/solution.py
+++ b/solution.py
@@ -118,10 +118,10 @@
             ).start()
         for u, p in enumerate(whole):
             pltpu.make_async_copy(ref.at[:, :, tile * depth + p], rxw.at[u, tile, w], rxw_recv.at[u]).start()
-    pltpu.make_async_copy(sbuf, sbuf, in_sem).wait()
 
     await_greetings(barrier, ns - 1)
     greet(known_sem.at[0])
+    pltpu.make_async_copy(sbuf, sbuf, in_sem).wait()
 
     def remote(src_ref, dst_ref, send_sem, recv_sem, device_id):
         pltpu.make_async_remote_copy(
@@ -183,6 +183,12 @@
         for k in range(1, nt):
             to = partner(tile, k, nt)
             guarded(when, to, lambda to=to: remote(cor, cbuf.at[tile], c_send, c_recv, {"tile": to}))
+
+    early = own
+
+    def early_half(when):
+        for u in early:
+            near_half(u, when, 1, 2)
 
     for level in (1, 2, 3):
         if level == 1:
@@ -200,12 +206,13 @@
         if level == 1:
             for u in range(2 * nb):
                 own_half(u)
-            for u in own:
-                near_half(u, None, 1, 2)
+        early_half(when)
         near_whole(0, when)
+        if level in (1,):
+            far_whole(1, when)
     for u in far[1:]:
-        near_half(u)
-    far_whole(1)
+        near_half(u, None, 1)
+    far_whole(1, lambda d: d > 1)
     near_whole(1)
     for u in own:
         near_half(u, None, 2)
@@ -222,10 +229,6 @@
         @pl.when(jnp.logical_not(edges[d][1]))
         def _(d=d):
             hx[d] = jnp.zeros((depth, 1, width), jnp.float32)
-
-        @pl.when(jnp.logical_not(faces[d][1]))
-        def _(d=d):
-            hz[d] = jnp.zeros((strip, width), jnp.float32)
 
     def edge_copy(d, p):
         return pltpu.make_async_remote_copy(
@@ -347,13 +350,19 @@
                 for h in range(halves):
                     hal[u, parity, pl.ds(2 * q + d, 1), pl.ds(h * LANES, LANES)] = total[q][h]
 
-    def gather_whole(u):
+    def receive_whole(u):
         pltpu.make_async_copy(rxw.at[u], rxw.at[u], rxw_recv.at[u]).wait()
         expand_whole(u)
+
+    def spread_whole(u):
         place_whole(u, other)
         for i in range(half_ns):
             remote(acc.at[u, 2 * i + other], r1.at[u, i], s1_send.at[u], s1_recv.at[u], twin)
         place_whole(u, core)
+
+    def gather_whole(u):
+        receive_whole(u)
+        spread_whole(u)
 
     def gather_half(u):
         got = rxh.at[u, 0, mine]
@@ -427,8 +436,10 @@
 
     def lateral(p):
         center = nrm[p]
-        before = jnp.where(row == 0, hx[0, p], pltpu.roll(center, 1, 0))
-        after = jnp.where(row == strip - 1, hx[1, p], pltpu.roll(center, strip - 1, 0))
+        above = 0.0 if p in whole else hx[0, p]
+        below = 0.0 if p in whole else hx[1, p]
+        before = jnp.where(row == 0, above, pltpu.roll(center, 1, 0))
+        after = jnp.where(row == strip - 1, below, pltpu.roll(center, strip - 1, 0))
         left = jnp.where(lanes == 0, 0.0, pltpu.roll(center, 1, 1))
         right = jnp.where(lanes == width - 1, 0.0, pltpu.roll(center, width - 1, 1))
         return before + after + left + right - 6.0 * center
@@ -437,22 +448,25 @@
         return [q for q in (p - 1, p + 1) if 0 <= q < depth]
 
     def base_plane(p, known):
-        if p in whole:
+        value = lateral(p)
+        for q in near_planes(p):
+            if q in known:
+                value = value + nrm[q]
+        out[p] = value
+
+    def add_outside():
+        for p in whole:
             for d in range(2):
                 @pl.when(edges[d][1])
                 def _(d=d):
                     edge_copy(d, p).wait_recv()
-        value = lateral(p)
-        for q in near_planes(p):
-            if q in known:
-                value = value + nrm[q]
-        for d in range(2):
-            if p == (depth - 1 if d else 0):
-                @pl.when(faces[d][1])
-                def _(d=d):
-                    face_copy(d).wait_recv()
-                value = value + hz[d]
-        out[p] = value
+            out[p, pl.ds(0, 1), :] = out[p, pl.ds(0, 1), :] + hx[0, p]
+            out[p, pl.ds(strip - 1, 1), :] = out[p, pl.ds(strip - 1, 1), :] + hx[1, p]
+        for d, p in ((0, 0), (1, depth - 1)):
+            @pl.when(faces[d][1])
+            def _(d=d, p=p):
+                face_copy(d).wait_recv()
+                out[p] = out[p] + hz[d]
 
     last = split[-1]
     middle = split[:-1]
@@ -465,7 +479,7 @@
     pltpu.make_async_copy(peers, peers, cy_recv).wait()
     half_corners = pltpu.make_async_copy(cby, csy, c_local.at[0])
     half_corners.start()
-    for u in own:
+    for u in early:
         relay(u, 1, 2)
     half_corners.wait()
 
@@ -474,15 +488,17 @@
     all_corners = pltpu.make_async_copy(cbuf, csm, c_local.at[1])
     all_corners.start()
     for u in far[1:]:
-        relay(u)
+        relay(u, 1)
     all_corners.wait()
     gather_whole(0)
     cross(0)
     stage2(0)
     for n in range(1, nb):
         gather_half(far[n])
+    receive_whole(1)
+    for n in range(1, nb):
         cross(n)
-    gather_whole(1)
+    spread_whole(1)
     relay(own[0], 2)
     stage2(1)
     for u in own[1:]:
@@ -501,6 +517,7 @@
     for p in near_planes(last):
         out[p] = out[p] + nrm[last]
     base_plane(last, known)
+    add_outside()
 
     for d in range(2):
         @pl.when(edges[d][0])

time: 33.1 us -> 33.1 us (level)
  no operation moved by 1% of the time
where the time goes in v4:
time: 33.1 us; the launch traced here: 32.8 us
  Pallas kernels  31.4 us (95%)
  local copies, waits for them, and re-layouts  1.38 us (4%)
    pallas_call x1, Pallas kernels, step(): pl.pallas_call(functools.partial(kernel, ns, nt), out_shape=jax.ShapeDtyp...  31.4 us
    unnamed x3, local copies, waits for them, and re-layouts  1.38 us

profile of v4, /device:TPU:1, one launch (start us, length us, event | category | flops | bytes accessed | tf_op | source)
XLA Modules:
  0.0 32.8 jit_solution(5937323602679498305)
XLA Ops:
  0.0 0.0 copy-start
  0.0 0.7 %copy-done = s32[2,2]{1,0:T(2,128)S(1)} copy-done((s32[2,2]{1,0:T(2,128)S(1)}, s32[2,2]{1,0:T(2,128)}, u32[]{:S(2)}) %copy-start) | copy-done | bytes 40
  0.7 31.4 %shard_map.37 = f32[4,64,256]{2,1,0:T(8,128)S(1)} custom-call(bf16[2,1,32,32,128]{4,3,2,1,0:T(8,128)(2,1)} %src.1, bf16[2,1,32,32,128]{4,3,2,1,0:T(8,128)(2,1)} %rcv.1, s32[2,2]{1,0:T(2,128)S(1)} %copy-done), custom_call_target="tpu_custom_call" | custom-call | tf_op jit(solution)/shard_map/pallas_call | solution.py:569
  32.1 0.7 %copy.5 = f32[4,64,256]{2,1,0:T(8,128)} copy(f32[4,64,256]{2,1,0:T(8,128)S(1)} %shard_map.37) | data formatting | bytes 524288
Async XLA Ops:
  0.0 0.7 %copy-start = (s32[2,2]{1,0:T(2,128)S(1)}, s32[2,2]{1,0:T(2,128)}, u32[]{:S(2)}) copy-start(s32[2,2]{1,0:T(2,128)} %cor.1) | copy-start | bytes 52

commit v5 on v4

--- a/solution.py
+++ b/solution.py
@@ -320,9 +320,9 @@
                     total[q][h] = piece if total[q][h] is None else total[q][h] + piece
         return total
 
-    def place_whole(u, parity):
+    def place_whole(u, parity, k, count):
         def one(n, carry):
-            j = 2 * (n // per_strip) + parity
+            j = 2 * lax.rem(pair + k + n // per_strip, half_ns) + parity
             at = lax.rem(n, per_strip) * block
             total = stack(whole_rows, j * strip + at, block)
             for q in range(2):
@@ -330,7 +330,7 @@
                     acc[u, j, q, pl.ds(at, block), pl.ds(h * LANES, LANES)] = total[q][h]
             return carry
 
-        lax.fori_loop(0, half_ns * per_strip, one, 0)
+        lax.fori_loop(0, count * per_strip, one, 0)
 
     def place_half(u, parity):
         top = (2 * pair + parity) * strip
@@ -355,10 +355,15 @@
         expand_whole(u)
 
     def spread_whole(u):
-        place_whole(u, other)
-        for i in range(half_ns):
-            remote(acc.at[u, 2 * i + other], r1.at[u, i], s1_send.at[u], s1_recv.at[u], twin)
-        place_whole(u, core)
+        for k in range(1, half_ns + 1):
+            i = lax.rem(pair + k, half_ns)
+            place_whole(u, other, k, 1)
+            remote(acc.at[u, 2 * i + other], r1.at[u, i], s1_send.at[u, k - 1], s1_recv.at[u, k - 1], twin)
+        place_whole(u, core, 1, half_ns)
+
+    def wait_first(u, k):
+        got = r1.at[u, lax.rem(pair + k, half_ns)]
+        pltpu.make_async_copy(got, got, s1_recv.at[u, k - 1]).wait()
 
     def gather_whole(u):
         receive_whole(u)
@@ -381,8 +386,8 @@
         pltpu.make_async_copy(hal1.at[u], hal1.at[u], h1_recv.at[u, 1]).wait()
 
     def stage2(u):
-        pltpu.make_async_copy(r1.at[u], r1.at[u], s1_recv.at[u]).wait()
         for k in range(1, half_ns):
+            wait_first(u, k)
             to = lax.rem(pair + k, half_ns)
             j = 2 * to + core
             acc[u, j] = acc[u, j] + r1[u, to]
@@ -398,6 +403,7 @@
 
     def finish_whole(u):
         p = whole[u]
+        wait_first(u, half_ns)
         pltpu.make_async_copy(r2.at[u], r2.at[u], s2_recv.at[u]).wait()
         image = acc[u, shot, 0] + r1[u, pair, 0]
         light = acc[u, shot, 1] + r1[u, pair, 1]
@@ -537,7 +543,8 @@
     drain(cby.at[pl.ds(1, half_ns - 1)], cy_send)
     for u in range(len(whole)):
         drain(rxw.at[u, pl.ds(0, nt - 1)], rxw_send.at[u])
-        drain(r1.at[u], s1_send.at[u])
+        for k in range(half_ns):
+            drain(r1.at[u, k], s1_send.at[u, k])
         drain(r2.at[u], s2_send.at[u])
     for u in range(2 * nb):
         drain(rxh.at[u, 0, pl.ds(0, half_nt - 1)], rxh_send.at[u])
@@ -609,8 +616,8 @@
                 dma,
                 dma,
                 dma((2,)),
-                dma((nw,)),
-                dma((nw,)),
+                dma((nw, half_ns)),
+                dma((nw, half_ns)),
                 dma((nw,)),
                 dma((nw,)),
                 dma((2 * nb, 2)),

time: 33.1 us -> 33.2 us (level)
  no operation moved by 1% of the time
where the time goes in v5:
time: 33.2 us; the launch traced here: 32.8 us
  Pallas kernels  31.4 us (95%)
  local copies, waits for them, and re-layouts  1.38 us (4%)
    pallas_call x1, Pallas kernels, step(): pl.pallas_call(functools.partial(kernel, ns, nt), out_shape=jax.ShapeDtyp...  31.4 us
    unnamed x3, local copies, waits for them, and re-layouts  1.38 us

profile of v5, /device:TPU:1, one launch (start us, length us, event | category | flops | bytes accessed | tf_op | source)
XLA Modules:
  0.0 32.8 jit_solution(6868060016563837671)
XLA Ops:
  0.0 0.0 copy-start
  0.0 0.7 %copy-done = s32[2,2]{1,0:T(2,128)S(1)} copy-done((s32[2,2]{1,0:T(2,128)S(1)}, s32[2,2]{1,0:T(2,128)}, u32[]{:S(2)}) %copy-start) | copy-done | bytes 40
  0.7 31.4 %shard_map.37 = f32[4,64,256]{2,1,0:T(8,128)S(1)} custom-call(bf16[2,1,32,32,128]{4,3,2,1,0:T(8,128)(2,1)} %src.1, bf16[2,1,32,32,128]{4,3,2,1,0:T(8,128)(2,1)} %rcv.1, s32[2,2]{1,0:T(2,128)S(1)} %copy-done), custom_call_target="tpu_custom_call" | custom-call | tf_op jit(solution)/shard_map/pallas_call | solution.py:576
  32.1 0.7 %copy.5 = f32[4,64,256]{2,1,0:T(8,128)} copy(f32[4,64,256]{2,1,0:T(8,128)S(1)} %shard_map.37) | data formatting | bytes 524288
Async XLA Ops:
  0.0 0.7 %copy-start = (s32[2,2]{1,0:T(2,128)S(1)}, s32[2,2]{1,0:T(2,128)}, u32[]{:S(2)}) copy-start(s32[2,2]{1,0:T(2,128)} %cor.1) | copy-start | bytes 52

commit v6 on v3

--- a/solution.py
+++ b/solution.py
@@ -118,10 +118,10 @@
             ).start()
         for u, p in enumerate(whole):
             pltpu.make_async_copy(ref.at[:, :, tile * depth + p], rxw.at[u, tile, w], rxw_recv.at[u]).start()
-    pltpu.make_async_copy(sbuf, sbuf, in_sem).wait()
 
     await_greetings(barrier, ns - 1)
     greet(known_sem.at[0])
+    pltpu.make_async_copy(sbuf, sbuf, in_sem).wait()
 
     def remote(src_ref, dst_ref, send_sem, recv_sem, device_id):
         pltpu.make_async_remote_copy(
@@ -183,6 +183,12 @@
         for k in range(1, nt):
             to = partner(tile, k, nt)
             guarded(when, to, lambda to=to: remote(cor, cbuf.at[tile], c_send, c_recv, {"tile": to}))
+
+    early = own
+
+    def early_half(when):
+        for u in early:
+            near_half(u, when, 1, 2)
 
     for level in (1, 2, 3):
         if level == 1:
@@ -200,12 +206,13 @@
         if level == 1:
             for u in range(2 * nb):
                 own_half(u)
-            for u in own:
-                near_half(u, None, 1, 2)
-        near_whole(0, when)
-    for u in far[1:]:
-        near_half(u)
-    far_whole(1)
+        early_half(when)
+        for u in far[1:]:
+            near_half(u, when)
+        if level in (1,):
+            far_whole(1, when)
+    near_whole(0)
+    far_whole(1, lambda d: d > 1)
     near_whole(1)
     for u in own:
         near_half(u, None, 2)
@@ -347,13 +354,19 @@
                 for h in range(halves):
                     hal[u, parity, pl.ds(2 * q + d, 1), pl.ds(h * LANES, LANES)] = total[q][h]
 
-    def gather_whole(u):
+    def receive_whole(u):
         pltpu.make_async_copy(rxw.at[u], rxw.at[u], rxw_recv.at[u]).wait()
         expand_whole(u)
+
+    def spread_whole(u):
         place_whole(u, other)
         for i in range(half_ns):
             remote(acc.at[u, 2 * i + other], r1.at[u, i], s1_send.at[u], s1_recv.at[u], twin)
         place_whole(u, core)
+
+    def gather_whole(u):
+        receive_whole(u)
+        spread_whole(u)
 
     def gather_half(u):
         got = rxh.at[u, 0, mine]
@@ -465,7 +478,7 @@
     pltpu.make_async_copy(peers, peers, cy_recv).wait()
     half_corners = pltpu.make_async_copy(cby, csy, c_local.at[0])
     half_corners.start()
-    for u in own:
+    for u in early:
         relay(u, 1, 2)
     half_corners.wait()
 
@@ -474,15 +487,17 @@
     all_corners = pltpu.make_async_copy(cbuf, csm, c_local.at[1])
     all_corners.start()
     for u in far[1:]:
-        relay(u)
+        relay(u, 1)
     all_corners.wait()
     gather_whole(0)
     cross(0)
     stage2(0)
     for n in range(1, nb):
         gather_half(far[n])
+    receive_whole(1)
+    for n in range(1, nb):
         cross(n)
-    gather_whole(1)
+    spread_whole(1)
     relay(own[0], 2)
     stage2(1)
     for u in own[1:]:

time: 33.1 us -> 33.1 us (level)
  no operation moved by 1% of the time
where the time goes in v6:
time: 33.1 us; the launch traced here: 32.8 us
  Pallas kernels  31.4 us (95%)
  local copies, waits for them, and re-layouts  1.38 us (4%)
    pallas_call x1, Pallas kernels, step(): pl.pallas_call(functools.partial(kernel, ns, nt), out_shape=jax.ShapeDtyp...  31.4 us
    unnamed x3, local copies, waits for them, and re-layouts  1.38 us

profile of v6, /device:TPU:1, one launch (start us, length us, event | category | flops | bytes accessed | tf_op | source)
XLA Modules:
  0.0 32.8 jit_solution(7096905380972203546)
XLA Ops:
  0.0 0.0 copy-start
  0.0 0.7 %copy-done = s32[2,2]{1,0:T(2,128)S(1)} copy-done((s32[2,2]{1,0:T(2,128)S(1)}, s32[2,2]{1,0:T(2,128)}, u32[]{:S(2)}) %copy-start) | copy-done | bytes 40
  0.7 31.4 %shard_map.37 = f32[4,64,256]{2,1,0:T(8,128)S(1)} custom-call(bf16[2,1,32,32,128]{4,3,2,1,0:T(8,128)(2,1)} %src.1, bf16[2,1,32,32,128]{4,3,2,1,0:T(8,128)(2,1)} %rcv.1, s32[2,2]{1,0:T(2,128)S(1)} %copy-done), custom_call_target="tpu_custom_call" | custom-call | tf_op jit(solution)/shard_map/pallas_call | solution.py:567
  32.1 0.7 %copy.5 = f32[4,64,256]{2,1,0:T(8,128)} copy(f32[4,64,256]{2,1,0:T(8,128)S(1)} %shard_map.37) | data formatting | bytes 524288
Async XLA Ops:
  0.0 0.7 %copy-start = (s32[2,2]{1,0:T(2,128)S(1)}, s32[2,2]{1,0:T(2,128)}, u32[]{:S(2)}) copy-start(s32[2,2]{1,0:T(2,128)} %cor.1) | copy-start | bytes 52
